TPU v7x, 32 devices: a whole 2x2x4 slice. The times are simulated.
32 devices in a mesh: row: 8 (over z, y), kk: 4 (over x, core).
Axes of the slice: x: 2, y: 2, z: 4, core: 2. Of those that a mesh axis runs over, the one named last changes fastest.
Arguments:
- left_blocks: bfloat16 [4096, 4096], P('row', 'kk'), may hold values from -6 to 6
- right_blocks: bfloat16 [4096, 1024], P('kk', 'row'), may hold values from -0.125 to 0.125
- left_mask: int32 [32, 32], P('row', 'kk'), may hold values 0 or 1
- right_mask: int32 [32, 8], P('kk', 'row'), may hold values 0 or 1
- out_mask: int32 [32, 8], P('row'), may hold values 0 or 1
Outputs:
- product_blocks: bfloat16 [4096, 1024], P(('row', 'kk'))
All inputs are finite; a program needn't handle non-finite values. No bound on the sum of `left_mask` or of `right_mask` or of `out_mask` on one device may be relied on, other than what follows from the above.
Results may differ from a plain program's by a relative error of at most 0.001.
Values may be sent and summed in bfloat16 or wider, within the bound.
A program may use at most 192 MiB of HBM per device.

v0:
```python
import jax
import jax.numpy as jnp
from jax import lax
from jax.sharding import PartitionSpec as P


def expand(mask, size):
    return jnp.repeat(jnp.repeat(mask, size, axis=0), size, axis=1)


def per_device(left_blocks, right_blocks, left_mask, right_mask, out_mask):
    block = left_blocks.shape[0] // left_mask.shape[0]
    left_used = left_blocks * expand(left_mask, block).astype(jnp.bfloat16)
    right_used = right_blocks * expand(right_mask, block).astype(jnp.bfloat16)
    share = left_used.shape[0] // lax.axis_size("kk")
    right_all = lax.all_gather(right_used, "row", axis=1, tiled=True)
    summed = lax.psum_scatter(
        jnp.dot(left_used, right_all, preferred_element_type=jnp.float32),
        "kk",
        scatter_dimension=0,
        tiled=True,
    )
    mask_rows = expand(out_mask, block).astype(jnp.float32)
    own_mask = lax.dynamic_slice_in_dim(mask_rows, lax.axis_index("kk") * share, share, 0)
    return (summed * own_mask).astype(jnp.bfloat16)


def solution(mesh):
    in_specs = (P("row", "kk"), P("kk", "row"), P("row", "kk"), P("kk", "row"), P("row", None))
    out_specs = P(("row", "kk"), None)
    return jax.shard_map(
        per_device, mesh=mesh, in_specs=in_specs, out_specs=out_specs, check_vma=False
    )
```

profile of v0, /device:TPU:0, one launch (start us, length us, event | category | flops | bytes accessed | tf_op | source)
XLA Modules:
  0.0 105.5 jit_solution(10613878520376923319)
XLA Ops:
  6.5 0.0 copy-start.1
  6.5 0.0 all-gather.2.cloned.1.call-start
  6.5 0.7 convert_bitcast_fusion
  7.3 0.1 broadcast_bitcast_fusion
  7.4 1.9 %broadcast_multiply_fusion = bf16[1024,128]{1,0:T(8,128)(2,1)} fusion(bf16[1024,128]{1,0:T(8,128)(2,1)} %param.6, bf16[1024]{0:T(1024)(128)(2,1)S(1)} %broadcast_bitcast_fusion), kind=kLoop, calls=%fused_computation.5 | loop fusion | flops 131072 | bytes 526336 | tf_op jit(solution)/shard_map/mul | solution.py:14
  9.2 0.0 all-gather.2.cloned.1.call-update
  9.2 0.0 reduce-scatter.2.cloned.1.call-start
  9.3 0.7 convert_element_type.36
  10.0 52.5 %all-gather.2.cloned.1.call-done = bf16[1024,1024]{1,0:T(8,128)(2,1)} async-done(((bf16[1024,128]{1,0:T(8,128)(2,1)}), bf16[1024,1024]{1,0:T(8,128)(2,1)}) %all-gather.2.cloned.1.call-update) | async-done | bytes 2097168 | tf_op jit(solution)/shard_map/all_gather | solution.py:16
  62.5 0.6 broadcast_in_dim.17
  63.1 0.0 copy-done.1
  63.1 4.2 %fusion = f32[512,1024]{1,0:T(8,128)} fusion(bf16[1024,1024]{1,0:T(8,128)(2,1)} %all-gather.2.cloned.1.call-done, bf16[512,1024]{1,0:T(8,128)(2,1)S(1)} %copy-done.1, bf16[64,8,8,128]{3,2,1,0:T(8,128)(2,1)S(1)} %bitcast.18), kind=kOutput, calls=%fused_computation.2 | convolution fusion | flops 1074266112 | bytes 6291456 | tf_op jit(solution)/shard_map/dot_general | solution.py:18
  67.3 0.0 copy-start
  67.3 0.0 reduce-scatter.2.cloned.1.call-update
  67.4 0.7 copy-done
  68.0 0.6 broadcast_in_dim.20
  68.6 0.5 copy.13
  69.1 27.7 %reduce-scatter.2.cloned.1.call-done = f32[128,1024]{1,0:T(8,128)} async-done(((f32[512,1024]{1,0:T(8,128)}), f32[128,1024]{1,0:T(8,128)}) %reduce-scatter.2.cloned.1.call-update) | async-done | bytes 524304 | tf_op jit(solution)/shard_map/reduce_scatter | solution.py:17
  96.8 1.8 %multiply_convert_fusion = bf16[128,1024]{1,0:T(8,128)(2,1)} fusion(f32[128,1024]{1,0:T(8,128)} %reduce-scatter.2.cloned.1.call-done, f32[512,1024]{1,0:T(8,128)S(1)} %bitcast.16, s32[]{:T(128)S(6)} %select_n.3), kind=kLoop, calls=%fused_computation.4 | loop fusion | flops 262144 | bytes 1310724 | tf_op jit(solution)/shard_map/convert_element_type | solution.py:25
  (3 shorter events, 0.0 us)
Async XLA Ops:
  6.5 56.6 %copy-start.1 = (bf16[512,1024]{1,0:T(8,128)(2,1)S(1)}, bf16[512,1024]{1,0:T(8,128)(2,1)}, u32[]{:S(2)}) copy-start(bf16[512,1024]{1,0:T(8,128)(2,1)} %param.5) | copy-start | bytes 3145732
  6.5 55.9 %all-gather.2.cloned.1.call-start = ((), (), s32[]{:S(2)}) async-start(), calls=%async_computation.1 | async-start | bytes 2359296 | tf_op jit(solution)/shard_map/all_gather | solution.py:16
  9.2 87.6 %reduce-scatter.2.cloned.1.call-start = ((), (), s32[]{:S(2)}) async-start(), calls=%async_computation.2 | async-start | bytes 2621440 | tf_op jit(solution)/shard_map/reduce_scatter | solution.py:17
  67.3 0.7 copy-start
Sparse Core Ops, SparseCore 0:
  9.4 53.0 all-gather.1
  67.5 29.3 reduce-scatter.1
where the time goes:
time: 106 us; the launch traced here: 105 us
  waiting for transfers between devices  80.3 us (76%)
  between operations  13.4 us (13%)
  other arithmetic  5.09 us (5%)
  matrix products  4.2 us (4%)
  local copies, waits for them, and re-layouts  2.44 us (2%)
    all_gather x1, waiting for transfers between devices, per_device(): right_all = lax.all_gather(right_used, 'row', axis=1, tiled=True)  52.5 us
    reduce_scatter x1, waiting for transfers between devices, per_device(): lax.psum_scatter(jnp.dot(left_used, right_all, preferred_element_type=jnp...  27.7 us
    dot_general x1, matrix products, per_device(): jnp.dot(left_used, right_all, preferred_element_type=jnp.float32)  4.2 us
  transfers between devices with their start and end apart: 2, of which 2 were waited for; matrix products, arithmetic and copies ran while one was open for 2% of the time, Pallas kernels for 0%

commit v1 on v0

v1 whole, which is shorter than its diff:
```python
import functools

import jax
import jax.numpy as jnp
from jax import lax
from jax.experimental import pallas as pl
from jax.experimental.pallas import tpu as pltpu
from jax.sharding import PartitionSpec as P

MESH = pl.DeviceIdType.MESH
PIECES = 4


def kernel(
    rows_n,
    kk_n,
    left_hbm,
    right_hbm,
    left_mask,
    right_mask,
    out_mask,
    out_ref,
    left_raw,
    right_raw,
    left,
    right_all,
    s1_out,
    s1_in,
    keep,
    s2_in,
    load_sem,
    recv_sem,
    line_sem,
    mate_sem,
    s1_send,
    s1_recv,
    s2_send,
    s2_recv,
):
    depth, cols = right_raw.shape
    share = out_ref.shape[0]
    block = left_raw.shape[0] // left_mask.shape[0]
    kblocks = left_mask.shape[1]
    outer = rows_n // 2
    peers = kk_n // 2
    piece = depth // PIECES

    row = lax.axis_index("row")
    kk = lax.axis_index("kk")
    o, i = row // 2, row % 2
    b, c = kk // 2, kk % 2
    has_up, has_down = o + 1 < outer, o >= 1
    mate = {"row": o * 2 + 1 - i}
    up, down = {"row": row + 2}, {"row": row - 2}
    partner = {"kk": b * 2 + 1 - c}

    def peer(j):
        return lax.rem(b + j, peers)

    load_right = pltpu.make_async_copy(right_hbm, right_raw, load_sem.at[0])
    load_left = pltpu.make_async_copy(left_hbm, left_raw, load_sem.at[1])
    load_right.start()
    load_left.start()

    barrier = pltpu.get_barrier_semaphore()

    def greet(device):
        pl.semaphore_signal(barrier, inc=1, device_id=device, device_id_type=MESH)

    greet(mate)
    greet(partner)
    for j in range(1, peers):
        greet({"kk": peer(j) * 2 + c})

    @pl.when(has_up)
    def _():
        greet(up)

    @pl.when(has_down)
    def _():
        greet(down)

    load_right.wait()
    for kb in range(kblocks):
        part = pl.ds(kb * block, block)
        scale = right_mask[kb, 0].astype(jnp.float32)
        right_all[row, part, :] = (right_raw[part, :].astype(jnp.float32) * scale).astype(jnp.bfloat16)

    pl.semaphore_wait(barrier, 1 + peers + has_up.astype(jnp.int32) + has_down.astype(jnp.int32))

    def gather_copy(slot, p, sem, device):
        ref = right_all.at[slot, pl.ds(p * piece, piece), :]
        return pltpu.make_async_remote_copy(
            src_ref=ref, dst_ref=ref, send_sem=sem, recv_sem=recv_sem.at[slot, p], device_id=device, device_id_type=MESH
        )

    def up_copy(slot, p):
        return gather_copy(slot, p, line_sem.at[slot, p], up)

    def down_copy(slot, p, at=None):
        return gather_copy(slot, p, line_sem.at[slot if at is None else at, p], down)

    def mate_copy(slot, p):
        return gather_copy(slot, p, mate_sem.at[slot, p], mate)

    def s1_copy(slot):
        return pltpu.make_async_remote_copy(
            src_ref=s1_out.at[slot], dst_ref=s1_in.at[slot], send_sem=s1_send.at[slot], recv_sem=s1_recv.at[slot],
            device_id=partner, device_id_type=MESH,
        )

    def s2_copy(slot, j):
        to = peer(j)
        return pltpu.make_async_remote_copy(
            src_ref=keep.at[slot, to], dst_ref=s2_in.at[slot, j - 1], send_sem=s2_send.at[slot, j - 1],
            recv_sem=s2_recv.at[slot, j - 1], device_id={"kk": to * 2 + c}, device_id_type=MESH,
        )

    def process(slot):
        block_in = right_all[slot]
        half = peers * share
        s1_out[slot] = jnp.dot(left[0:half, :], block_in, preferred_element_type=jnp.float32)
        s1_copy(slot).start()
        got = jnp.dot(left[half : 2 * half, :], block_in, preferred_element_type=jnp.float32)
        for t in range(peers):
            keep[slot, t] = got[t * share : (t + 1) * share]

    def combine1(slot):
        s1_copy(slot).wait_recv()
        for t in range(peers):
            keep[slot, t] = keep[slot, t] + s1_in[slot, t * share : (t + 1) * share]
        for j in range(1, peers):
            s2_copy(slot, j).start()

    def combine2(slot):
        total = keep[slot, b]
        for j in range(1, peers):
            s2_copy(slot, j).wait_recv()
            total = total + s2_in[slot, j - 1]
        per = cols // block
        own = kk * share // block
        at = pl.multiple_of(slot * cols, cols)
        scale = out_mask[own, slot * per].astype(jnp.float32)
        out_ref[:, pl.ds(at, cols)] = (total * scale).astype(jnp.bfloat16)

    def ordered(n):
        low = jnp.minimum(o, outer - 1 - o)
        near = (n + 1) // 2
        paired = o + jnp.where(n % 2 == 1, -near, near)
        far = n - low
        single = o + jnp.where(o < outer - 1 - o, far, -far)
        return jnp.where(n <= 2 * low, paired, single)

    def mate_slot(n):
        return ordered(n) * 2 + 1 - i

    for p in range(PIECES):
        mate_copy(row, p).start()

        @pl.when(has_up)
        def _():
            up_copy(row, p).start()

        @pl.when(has_down)
        def _():
            down_copy(row, p, rows_n).start()

    load_left.wait()
    for s in range(2):
        for t in range(peers):
            src = pl.multiple_of((2 * t + (1 - c if s == 0 else c)) * share, share)
            dst = (s * peers + t) * share
            for q in range(share // block):
                for kb in range(kblocks):
                    scale = left_mask[src // block + q, kb].astype(jnp.float32)
                    lanes = pl.ds(kb * block, block)
                    tile = left_raw[pl.ds(pl.multiple_of(src + q * block, block), block), lanes]
                    left[dst + q * block : dst + (q + 1) * block, kb * block : (kb + 1) * block] = (
                        tile.astype(jnp.float32) * scale
                    ).astype(jnp.bfloat16)

    process(row)
    combine1(row)

    def at_distance(d, low_fn, high_fn):
        @pl.when(o - d >= 0)
        def _():
            low_fn(row - 2 * d)

        @pl.when((o + d < outer) & (d >= 1))
        def _():
            high_fn(row + 2 * d)

    def both(d, fn):
        at_distance(d, fn, fn)

    def tick(d, carry):
        for p in range(PIECES):

            def from_low(slot):
                mate_copy(slot, p).wait_recv()

                @pl.when(has_up)
                def _():
                    up_copy(slot, p).start()

                mate_copy(slot, p).start()

            def from_high(slot):
                mate_copy(slot, p).wait_recv()

                @pl.when(has_down)
                def _():
                    down_copy(slot, p).start()

                mate_copy(slot, p).start()

            at_distance(d, from_low, from_high)
        both(d, process)
        mslot = mate_slot(d - 1)
        for p in range(PIECES):
            mate_copy(mslot, p).wait_recv()
        process(mslot)
        both(d, combine1)
        combine1(mslot)
        both(d - 1, combine2)

        @pl.when(d >= 2)
        def _():
            combine2(mate_slot(d - 2))

        return carry

    lax.fori_loop(1, outer, tick, 0)

    last = mate_slot(outer - 1)
    for p in range(PIECES):
        mate_copy(last, p).wait_recv()
    process(last)
    both(outer - 1, combine2)
    if outer >= 2:
        combine2(mate_slot(outer - 2))
    combine1(last)
    combine2(last)

    def drain(slot, carry):
        s1_copy(slot).wait_send()
        for j in range(1, peers):
            s2_copy(slot, j).wait_send()
        so = slot // 2

        @pl.when(slot % 2 == i)
        def _():
            for p in range(PIECES):
                mate_copy(slot, p).wait_send()

                @pl.when(has_up & (so <= o))
                def _():
                    up_copy(slot, p).wait_send()

                @pl.when(has_down & (so > o))
                def _():
                    down_copy(slot, p).wait_send()

        return carry

    lax.fori_loop(0, rows_n, drain, 0)

    @pl.when(has_down)
    def _():
        for p in range(PIECES):
            down_copy(row, p, rows_n).wait_send()


def per_device(rows_n, kk_n, left_blocks, right_blocks, left_mask, right_mask, out_mask):
    rows = left_blocks.shape[0]
    depth, cols = right_blocks.shape
    share = rows // kk_n
    peers = kk_n // 2
    half = peers * share
    dma = pltpu.SemaphoreType.DMA
    f32, bf16 = jnp.float32, jnp.bfloat16
    return pl.pallas_call(
        functools.partial(kernel, rows_n, kk_n),
        out_shape=jax.ShapeDtypeStruct((share, rows_n * cols), bf16),
        in_specs=[pl.BlockSpec(memory_space=pl.ANY)] * 2 + [pl.BlockSpec(memory_space=pltpu.SMEM)] * 3,
        out_specs=pl.BlockSpec(memory_space=pltpu.VMEM),
        scratch_shapes=[
            pltpu.VMEM((rows, depth), bf16),
            pltpu.VMEM((depth, cols), bf16),
            pltpu.VMEM((rows, depth), bf16),
            pltpu.VMEM((rows_n, depth, cols), bf16),
            pltpu.VMEM((rows_n, half, cols), f32),
            pltpu.VMEM((rows_n, half, cols), f32),
            pltpu.VMEM((rows_n, peers, share, cols), f32),
            pltpu.VMEM((rows_n, max(peers - 1, 1), share, cols), f32),
            dma((2,)),
            dma((rows_n, PIECES)),
            dma((rows_n + 1, PIECES)),
            dma((rows_n, PIECES)),
            dma((rows_n,)),
            dma((rows_n,)),
            dma((rows_n, max(peers - 1, 1))),
            dma((rows_n, max(peers - 1, 1))),
        ],
        compiler_params=pltpu.CompilerParams(
            collective_id=0, has_side_effects=True, vmem_limit_bytes=62 * 1024 * 1024
        ),
    )(left_blocks, right_blocks, left_mask, right_mask, out_mask)


def solution(mesh):
    in_specs = (P("row", "kk"), P("kk", "row"), P("row", "kk"), P("kk", "row"), P("row", None))
    out_specs = P(("row", "kk"), None)
    body = functools.partial(per_device, mesh.shape["row"], mesh.shape["kk"])
    return jax.shard_map(body, mesh=mesh, in_specs=in_specs, out_specs=out_specs, check_vma=False)
```

time: 106 us -> 39.1 us (0.37)
  waiting for transfers between devices: 80.3 us -> 0 us
  Pallas kernels: 0 us -> 35.9 us
  between operations: 13.4 us -> 0.01 us
  other arithmetic: 5.09 us -> 0 us
  matrix products: 4.2 us -> 0 us
    all_gather x1 -> x0, waiting for transfers between devices: 52.5 us -> none  [per_device(): right_all = lax.all_gather(right_used, 'row', axis=1, tiled=True)]
    pallas_call x0 -> x1, Pallas kernels: none -> 35.9 us  [per_device(): pl.pallas_call(functools.partial(kernel, rows_n, kk_n), out_shape=jax.Sha...]
    reduce_scatter x1 -> x0, waiting for transfers between devices: 27.7 us -> none  [per_device(): lax.psum_scatter(jnp.dot(left_used, right_all, preferred_element_type=jnp...]
    dot_general x1 -> x0, matrix products: 4.2 us -> none  [per_device(): jnp.dot(left_used, right_all, preferred_element_type=jnp.float32)]
    convert_element_type x4 -> x0, other arithmetic: 3.24 us -> none  [the longest x1 1.8 us: per_device(): return (summed * own_mask).astype(jnp.bfloat16)]
    unnamed x5 -> x2, local copies, waits for them, and re-layouts: 1.13 us -> 2.99 us
    mul x1 -> x0, other arithmetic: 1.86 us -> none  [per_device(): right_used = right_blocks * expand(right_mask, block).astype(jnp.bfloat16)]
    broadcast_in_dim x4 -> x0, local copies, waits for them, and re-layouts: 1.24 us -> none  [expand(): return jnp.repeat(jnp.repeat(mask, size, axis=0), size, axis=1)]
  transfers between devices with their start and end apart: 2 -> 0, of which waited for: 2 -> 0; matrix products, arithmetic and copies ran while one was open for 2% -> 0% of each run, Pallas kernels for 0% -> 0%
where the time goes in v1:
time: 39.1 us; the launch traced here: 38.9 us
  Pallas kernels  35.9 us (92%)
  local copies, waits for them, and re-layouts  2.99 us (8%)
    pallas_call x1, Pallas kernels, per_device(): pl.pallas_call(functools.partial(kernel, rows_n, kk_n), out_shape=jax.Sha...  35.9 us
    unnamed x2, local copies, waits for them, and re-layouts  2.99 us

profile of v1, /device:TPU:0, one launch (start us, length us, event | category | flops | bytes accessed | tf_op | source)
XLA Modules:
  0.0 38.9 jit_solution(6186957545886073654)
XLA Ops:
  0.0 1.3 %copy.6.right_mask = s32[8,1]{1,0:T(8,128)} copy(s32[8,1]{0,1:T(1,128)} %param.8) | data formatting | bytes 64 | tf_op args[3]
  1.3 35.9 %shard_map.55 = bf16[128,1024]{1,0:T(8,128)(2,1)} custom-call(bf16[512,1024]{1,0:T(8,128)(2,1)} %left_hbm.1, bf16[1024,128]{1,0:T(8,128)(2,1)} %right_hbm.1, s32[4,8]{1,0:T(4,128)} %left_mask.1, s32[8,1]{1,0:T(8,128)} %copy.6.right_mask, s32[4,8]{1,0:T(4,128)} %out_mask.1), custom_call_target="tpu_custom_call" | custom-call | tf_op jit(solution)/shard_map/pallas_call | solution.py:283
  37.2 1.7 %copy.8 = bf16[128,1024]{1,0:T(8,128)(2,1)} copy(bf16[128,1024]{1,0:T(8,128)(2,1)} %shard_map.55) | data formatting | bytes 524288

commit v2 on v1

--- a/solution.py
+++ b/solution.py
@@ -8,7 +8,7 @@
 from jax.sharding import PartitionSpec as P
 
 MESH = pl.DeviceIdType.MESH
-PIECES = 4
+PIECES = 2
 
 
 def kernel(
@@ -83,7 +83,7 @@
     load_right.wait()
     for kb in range(kblocks):
         part = pl.ds(kb * block, block)
-        scale = right_mask[kb, 0].astype(jnp.float32)
+        scale = right_mask[kb].astype(jnp.float32)
         right_all[row, part, :] = (right_raw[part, :].astype(jnp.float32) * scale).astype(jnp.bfloat16)
 
     pl.semaphore_wait(barrier, 1 + peers + has_up.astype(jnp.int32) + has_down.astype(jnp.int32))
@@ -237,10 +237,10 @@
     for p in range(PIECES):
         mate_copy(last, p).wait_recv()
     process(last)
+    combine1(last)
     both(outer - 1, combine2)
     if outer >= 2:
         combine2(mate_slot(outer - 2))
-    combine1(last)
     combine2(last)
 
     def drain(slot, carry):
@@ -306,7 +306,7 @@
         compiler_params=pltpu.CompilerParams(
             collective_id=0, has_side_effects=True, vmem_limit_bytes=62 * 1024 * 1024
         ),
-    )(left_blocks, right_blocks, left_mask, right_mask, out_mask)
+    )(left_blocks, right_blocks, left_mask, right_mask.reshape(-1), out_mask)
 
 
 def solution(mesh):

time: 39.1 us -> 36.7 us (0.939)
  local copies, waits for them, and re-layouts: 2.99 us -> 1.67 us
  Pallas kernels: 35.9 us -> 34.8 us
    unnamed x2 -> x1, local copies, waits for them, and re-layouts: 2.99 us -> 1.67 us
    pallas_call x1, Pallas kernels: 35.9 us -> 34.8 us  [per_device(): pl.pallas_call(functools.partial(kernel, rows_n, kk_n), out_shape=jax.Sha...]
where the time goes in v2:
time: 36.7 us; the launch traced here: 36.5 us
  Pallas kernels  34.8 us (95%)
  local copies, waits for them, and re-layouts  1.67 us (5%)
    pallas_call x1, Pallas kernels, per_device(): pl.pallas_call(functools.partial(kernel, rows_n, kk_n), out_shape=jax.Sha...  34.8 us
    unnamed x1, local copies, waits for them, and re-layouts  1.67 us

profile of v2, /device:TPU:0, one launch (start us, length us, event | category | flops | bytes accessed | tf_op | source)
XLA Modules:
  0.0 36.5 jit_solution(3570420243983357090)
XLA Ops:
  0.0 34.8 %shard_map.55 = bf16[128,1024]{1,0:T(8,128)(2,1)} custom-call(bf16[512,1024]{1,0:T(8,128)(2,1)} %left_hbm.1, bf16[1024,128]{1,0:T(8,128)(2,1)} %right_hbm.1, s32[4,8]{1,0:T(4,128)} %left_mask.1, s32[8]{0:T(128)} %bitcast.1, s32[4,8]{1,0:T(4,128)} %out_mask.1), custom_call_target="tpu_custom_call" | custom-call | tf_op jit(solution)/shard_map/pallas_call | solution.py:283
  34.8 1.7 %copy.7 = bf16[128,1024]{1,0:T(8,128)(2,1)} copy(bf16[128,1024]{1,0:T(8,128)(2,1)} %shard_map.55) | data formatting | bytes 524288

commit v3 on v2

--- a/solution.py
+++ b/solution.py
@@ -9,6 +9,8 @@
 
 MESH = pl.DeviceIdType.MESH
 PIECES = 2
+VMEM_BYTES = 67043328
+SPARE = 256 * 1024
 
 
 def kernel(
@@ -89,7 +91,8 @@
     pl.semaphore_wait(barrier, 1 + peers + has_up.astype(jnp.int32) + has_down.astype(jnp.int32))
 
     def gather_copy(slot, p, sem, device):
-        ref = right_all.at[slot, pl.ds(p * piece, piece), :]
+        first = depth * 3 // 8
+        ref = right_all.at[slot, pl.ds(p * first, first if p == 0 else depth - first), :]
         return pltpu.make_async_remote_copy(
             src_ref=ref, dst_ref=ref, send_sem=sem, recv_sem=recv_sem.at[slot, p], device_id=device, device_id_type=MESH
         )
@@ -282,7 +285,7 @@
     f32, bf16 = jnp.float32, jnp.bfloat16
     return pl.pallas_call(
         functools.partial(kernel, rows_n, kk_n),
-        out_shape=jax.ShapeDtypeStruct((share, rows_n * cols), bf16),
+        out_shape=pltpu.VMEM((share, rows_n * cols), bf16),
         in_specs=[pl.BlockSpec(memory_space=pl.ANY)] * 2 + [pl.BlockSpec(memory_space=pltpu.SMEM)] * 3,
         out_specs=pl.BlockSpec(memory_space=pltpu.VMEM),
         scratch_shapes=[
@@ -304,7 +307,7 @@
             dma((rows_n, max(peers - 1, 1))),
         ],
         compiler_params=pltpu.CompilerParams(
-            collective_id=0, has_side_effects=True, vmem_limit_bytes=62 * 1024 * 1024
+            collective_id=0, has_side_effects=True, vmem_limit_bytes=VMEM_BYTES - share * rows_n * cols * 2 - SPARE
         ),
     )(left_blocks, right_blocks, left_mask, right_mask.reshape(-1), out_mask)
 

time: 36.7 us -> 35 us (0.954)
  local copies, waits for them, and re-layouts: 1.67 us -> 0.71 us
  Pallas kernels: 34.8 us -> 34.1 us
    unnamed x1, local copies, waits for them, and re-layouts: 1.67 us -> 0.71 us
    pallas_call x1, Pallas kernels: 34.8 us -> 34.1 us  [per_device(): pl.pallas_call(functools.partial(kernel, rows_n, kk_n), out_shape=pltpu.V...]
where the time goes in v3:
time: 35 us; the launch traced here: 34.8 us
  Pallas kernels  34.1 us (97%)
  local copies, waits for them, and re-layouts  0.71 us (2%)
    pallas_call x1, Pallas kernels, per_device(): pl.pallas_call(functools.partial(kernel, rows_n, kk_n), out_shape=pltpu.V...  34.1 us
    unnamed x1, local copies, waits for them, and re-layouts  0.71 us

profile of v3, /device:TPU:0, one launch (start us, length us, event | category | flops | bytes accessed | tf_op | source)
XLA Modules:
  0.0 34.8 jit_solution(5438176074500828007)
XLA Ops:
  0.0 34.1 %shard_map.55 = bf16[128,1024]{1,0:T(8,128)(2,1)S(1)} custom-call(bf16[512,1024]{1,0:T(8,128)(2,1)} %left_hbm.1, bf16[1024,128]{1,0:T(8,128)(2,1)} %right_hbm.1, s32[4,8]{1,0:T(4,128)} %left_mask.1, s32[8]{0:T(128)} %bitcast.1, s32[4,8]{1,0:T(4,128)} %out_mask.1), custom_call_target="tpu_custom_call" | custom-call | tf_op jit(solution)/shard_map/pallas_call | solution.py:286
  34.1 0.7 %copy.7 = bf16[128,1024]{1,0:T(8,128)(2,1)} copy(bf16[128,1024]{1,0:T(8,128)(2,1)S(1)} %shard_map.55) | data formatting | bytes 524288
